TPU v7x, 128 devices: a whole 4x4x4 slice. The times are simulated.
128 devices in a mesh: grp: 8 (over y, core), loc: 16 (over x, z).
Axes of the slice: x: 4, y: 4, z: 4, core: 2. Of those that a mesh axis runs over, the one named last changes fastest.
Arguments:
- tokens: bfloat16 [32768, 1024], P(('grp', 'loc')), may hold values from -6 to 6
- w_gate: bfloat16 [128, 1024, 2816], P(('grp', 'loc')), may hold values from -0.1875 to 0.1875
- w_up: bfloat16 [128, 1024, 2816], P(('grp', 'loc')), may hold values from -0.1875 to 0.1875
- w_down: bfloat16 [128, 2816, 1024], P(('grp', 'loc')), may hold values from -0.109375 to 0.109375
- chosen: int32 [128, 512], replicated, may hold values from -1 to 32767, as said below
- gate_weights: float32 [128, 512], replicated, may hold values from 0.05 to 1
Outputs:
- combined: bfloat16 [32768, 1024], P(('grp', 'loc'))
Inputs may be any that keep to these rules, and one draw needn't show every extreme that they name: `chosen`: each entry is a token index or -1 for an empty slot, empty slots anywhere in a row. One expert's row names a token at most once. At most 8 entries of one expert's row lie among the 256 tokens of one device, and every expert has exactly 8 from some device. Some expert has no empty slot.
All inputs are finite; a program needn't handle non-finite values.
Results may differ from a plain program's by a relative error of at most 0.0085.
Values may be sent and summed in bfloat16 or wider, within the bound.
A program may use at most 128 MiB of HBM per device.

v0:
```python
import jax
import jax.numpy as jnp
from jax import lax
from jax.sharding import PartitionSpec as P

PAIR_MOST = 8


def in_blocks(array, dim, count):
    before, after = (array.shape[:dim], array.shape[dim + 1 :])
    return jnp.moveaxis(array.reshape(*before, count, -1, *after), dim, 0)


def joined_along(pieces, dim):
    shape = list(pieces.shape[1:])
    shape[dim] *= pieces.shape[0]
    return jnp.moveaxis(pieces, 0, dim).reshape(shape)


def one_exchange(array, axis, axes, splits, concats):
    sizes = [lax.axis_size(a) for a in axes]
    pieces = in_blocks(array, splits[0], sizes[0])
    pieces = jnp.moveaxis(in_blocks(pieces, splits[1] + 1, sizes[1]), 0, 1)
    inside = pieces.shape[2:]
    pieces = pieces.reshape(-1, *inside)
    pieces = lax.all_to_all(pieces, axis, split_axis=0, concat_axis=0, tiled=True)
    pieces = joined_along(pieces.reshape(*sizes, *inside), concats[0] + 1)
    return joined_along(pieces, concats[1])


def expert_apply(row_block, w_gate, w_up, w_down):
    gate_pre = jnp.dot(row_block, w_gate[0], preferred_element_type=jnp.float32)
    up_pre = jnp.dot(row_block, w_up[0], preferred_element_type=jnp.float32)
    hidden = (jax.nn.silu(gate_pre) * up_pre).astype(jnp.bfloat16)
    produced = jnp.dot(hidden, w_down[0], preferred_element_type=jnp.float32).astype(jnp.bfloat16)
    return produced


def strict_lower(length):
    row_iota = lax.broadcasted_iota(jnp.int32, (length, length), 0)
    col_iota = lax.broadcasted_iota(jnp.int32, (length, length), 1)
    return (col_iota < row_iota).astype(jnp.float32)


def compact_apply(received, chosen_row, token_count, w_gate, w_up, w_down):
    devices, slot_count, model_width = received.shape
    slot_total = chosen_row.shape[0]
    is_live = chosen_row >= 0
    source = jnp.where(is_live, chosen_row // token_count, 0)
    onehot = ((source[:, None] == jnp.arange(devices)[None, :]) & is_live[:, None]).astype(
        jnp.float32
    )
    before = jnp.dot(strict_lower(slot_total), onehot)
    slot_rank = jnp.sum(before * onehot, axis=1).astype(jnp.int32)
    position = source * slot_count + slot_rank
    flat_iota = lax.broadcasted_iota(jnp.int32, (slot_total, devices * slot_count), 1)
    place_table = ((position[:, None] == flat_iota) & is_live[:, None]).astype(jnp.bfloat16)
    flat_rows = received.reshape(devices * slot_count, model_width)
    gathered = jnp.dot(place_table, flat_rows, preferred_element_type=jnp.float32).astype(
        jnp.bfloat16
    )
    produced = expert_apply(gathered, w_gate, w_up, w_down)
    placed = lax.dot_general(
        place_table, produced, (((0,), (0,)), ((), ())), preferred_element_type=jnp.float32
    )
    return placed.astype(jnp.bfloat16).reshape(devices, slot_count, model_width)


def shards(tokens, w_gate, w_up, w_down, chosen, gate_weights):
    group_count = lax.axis_size("grp")
    local_count = lax.axis_size("loc")
    device_id = lax.axis_index("grp") * local_count + lax.axis_index("loc")
    token_count, model_width = tokens.shape
    experts, slot_total = chosen.shape
    slot_count = PAIR_MOST
    is_live = chosen >= 0
    is_mine = is_live & (chosen // token_count == device_id)
    mine_float = is_mine.astype(jnp.float32)
    slot_rank = lax.dot_general(mine_float, strict_lower(slot_total), (((1,), (1,)), ((), ())))
    rank_table = (
        (slot_rank.astype(jnp.int32)[:, :, None] == jnp.arange(slot_count)[None, None, :])
        & is_mine[:, :, None]
    ).astype(jnp.float32)
    local_index = jnp.where(is_mine, chosen - device_id * token_count, 0).astype(jnp.float32)
    pick_local = jnp.sum(rank_table * local_index[:, :, None], axis=1)
    pick_present = jnp.sum(rank_table, axis=1)
    pick_weight = jnp.sum(rank_table * gate_weights[:, :, None], axis=1)
    pick_index = jnp.where(pick_present > 0.5, pick_local.astype(jnp.int32), -1)
    token_iota = lax.broadcasted_iota(jnp.int32, (experts, slot_count, token_count), 2)
    select_table = pick_index[:, :, None] == token_iota
    outgoing = jnp.einsum(
        "ept,td->epd", select_table.astype(jnp.bfloat16), tokens, preferred_element_type=jnp.float32
    ).astype(jnp.bfloat16)
    stacked = outgoing.reshape(group_count, local_count, slot_count, model_width)
    arrived = one_exchange(stacked, ("grp", "loc"), ("grp", "loc"), (0, 1), (0, 1))
    own_row = lax.dynamic_index_in_dim(chosen, device_id, 0, keepdims=False)
    produced = compact_apply(
        arrived.reshape(experts, slot_count, model_width),
        own_row,
        token_count,
        w_gate,
        w_up,
        w_down,
    )
    produced = produced.reshape(group_count, local_count, slot_count, model_width)
    returned = one_exchange(produced, ("grp", "loc"), ("grp", "loc"), (0, 1), (0, 1))
    returned = returned.reshape(experts, slot_count, model_width)
    mixing = (select_table.astype(jnp.float32) * pick_weight[:, :, None]).reshape(
        experts * slot_count, token_count
    )
    flat_back = returned.reshape(experts * slot_count, model_width).astype(jnp.float32)
    summed = lax.dot_general(
        mixing, flat_back, (((0,), (0,)), ((), ())), preferred_element_type=jnp.float32
    )
    return summed.astype(jnp.bfloat16)


def solution(mesh):
    return jax.shard_map(
        shards,
        mesh=mesh,
        in_specs=(
            P(("grp", "loc"), None),
            P(("grp", "loc"), None, None),
            P(("grp", "loc"), None, None),
            P(("grp", "loc"), None, None),
            P(),
            P(),
        ),
        out_specs=P(("grp", "loc"), None),
        check_vma=False,
    )
```

profile of v0, /device:TPU:1, one launch (start us, length us, event | category | flops | bytes accessed | tf_op | source)
XLA Modules:
  0.0 110.0 jit_solution(2321053731984799351)
XLA Ops:
  0.0 0.0 copy-start
  0.0 1.2 %select_convert_fusion = (f32[128,512]{1,0:T(8,128)S(1)}, pred[128,512]{1,0:T(32,128)(4,1)S(1)}) fusion(s32[128,512]{1,0:T(8,128)} %param.10, s32[]{:T(128)S(6)} %mul.51, s32[]{:T(128)S(6)} %add.27), kind=kLoop, calls=%fused_computation.46 | loop fusion | flops 1376256 | bytes 589832 | tf_op jit(solution)/shard_map/convert_element_type | solution.py:84
  1.3 0.3 convolution_convert_fusion
  1.6 2.0 %select_reduce_fusion = (bf16[128,8]{1,0:T(8,128)(2,1)S(1)}, f32[128,8]{1,0:T(8,128)S(1)}, f32[128,8]{1,0:T(8,128)S(1)}) fusion(f32[128,512]{1,0:T(8,128)} %param.11, s32[128,512]{1,0:T(8,128)S(1)} %convolution_convert_fusion, pred[128,512]{1,0:T(8,128)(4,1)S(1)} %copy.19, f32[128,512]{1,0:T(8,128)S(1)} %get-tuple-element.8), kind=kLoop, calls=%fused_computation.14 | loop fusion | flops 4191232 | bytes 862208 | tf_op jit(solution)/shard_map/reduce_sum | solution.py:87
  3.6 0.2 iota_compare_fusion.2
  3.8 0.0 copy-done
  3.8 0.7 convert_bitcast_fusion.1
  4.5 2.5 %copy.13 = bf16[128,1,1,8,1024]{4,3,2,1,0:T(8,128)(2,1)} copy(bf16[128,1,1,8,1024]{4,0,3,2,1:T(8,128)(2,1)S(1)} %convert_bitcast_fusion.1) | data formatting | bytes 4194304 | tf_op jit(solution)/shard_map/reshape;transpose;transpose;reshape;reshape;reshape | solution.py:25
  7.0 11.5 %all-to-all-start = ((bf16[128,1,1,8,1024]{4,3,2,1,0:T(8,128)(2,1)}), bf16[128,1,1,8,1024]{4,3,2,1,0:T(8,128)(2,1)S(1)}, u32[]{:S(2)}, u32[]{:S(2)}) async-start(bf16[128,1,1,8,1024]{4,3,2,1,0:T(8,128)(2,1)} %copy.13), calls=%async_computation | async-start | bytes 4194304 | tf_op jit(solution)/shard_map/all_to_all | solution.py:26
  18.5 0.7 constant_dynamic-slice_fusion
  19.3 0.3 fusion.34
  19.6 28.5 %all-to-all-done = bf16[128,1,1,8,1024]{4,3,2,1,0:T(8,128)(2,1)S(1)} async-done(((bf16[128,1,1,8,1024]{4,3,2,1,0:T(8,128)(2,1)}), bf16[128,1,1,8,1024]{4,3,2,1,0:T(8,128)(2,1)S(1)}, u32[]{:S(2)}, u32[]{:S(2)}) %all-to-all-start) | async-done | bytes 2097184 | tf_op jit(solution)/shard_map/all_to_all | solution.py:26
  48.2 1.3 %fusion.26 = bf16[512,1024]{1,0:T(8,128)(2,1)S(1)} fusion(bf16[128,1,1,8,1024]{4,3,2,1,0:T(8,128)(2,1)S(1)} %all-to-all-done, s32[512]{0:T(512)S(1)} %convert_add_fusion, pred[512]{0:T(512)(128)(4,1)S(1)} %broadcast_compare_fusion), kind=kOutput, calls=%fused_computation.22 | convolution fusion | flops 1075314688 | bytes 3148288 | tf_op jit(solution)/shard_map/dot_general | solution.py:59
  49.5 0.0 copy-start.1
  49.5 1.0 copy-done.1
  50.4 7.6 %fusion.4 = f32[512,2816]{1,0:T(8,128)} fusion(bf16[512,1024]{1,0:T(8,128)(2,1)S(1)} %fusion.26, bf16[1,1024,2816]{2,1,0:T(8,128)(2,1)} %param.7), kind=kOutput, calls=%fused_computation.4 | convolution fusion | flops 2952790016 | bytes 12582912 | tf_op jit(solution)/shard_map/dot_general | solution.py:32
  58.1 13.4 %fusion.21 = bf16[512,1024]{1,0:T(8,128)(2,1)} fusion(bf16[1,2816,1024]{2,1,0:T(8,128)(2,1)} %param.9, f32[512,2816]{1,0:T(8,128)} %fusion.4, bf16[512,1024]{1,0:T(8,128)(2,1)} %copy-done.1, bf16[1,1024,2816]{2,1,0:T(8,128)(2,1)} %param.8), kind=kOutput, calls=%fused_computation.21 | convolution fusion | flops 5914755072 | bytes 19398656 | tf_op jit(solution)/shard_map/dot_general | solution.py:35
  71.5 2.6 %convert_bitcast_fusion = bf16[128,1,1,8,1024]{4,3,2,1,0:T(8,128)(2,1)S(1)} fusion(bf16[512,1024]{1,0:T(8,128)(2,1)} %fusion.21, s32[512]{0:T(512)S(1)} %convert_add_fusion, pred[512]{0:T(512)(128)(4,1)S(1)} %broadcast_compare_fusion), kind=kOutput, calls=%fused_computation.11 | convolution fusion | flops 1075838976 | bytes 3148288 | tf_op jit(solution)/shard_map/dot_general | solution.py:63
  74.1 34.1 %all_to_all.10 = bf16[128,1,1,8,1024]{4,3,2,1,0:T(8,128)(2,1)S(1)} all-to-all(bf16[128,1,1,8,1024]{4,3,2,1,0:T(8,128)(2,1)S(1)} %convert_bitcast_fusion), channel_id=1, replica_groups=mesh['grp'=8,'loc'=16] {'grp','loc'}, dimensions={0} | all-to-all | bytes 4194304 | tf_op jit(solution)/shard_map/all_to_all | solution.py:26
  108.2 1.8 %fusion.31 = bf16[256,1024]{1,0:T(8,128)(2,1)} fusion(bf16[128,1,1,8,1024]{4,3,2,1,0:T(8,128)(2,1)S(1)} %all_to_all.10, bf16[128,8]{1,0:T(8,128)(2,1)S(1)} %get-tuple-element.5, s32[128,8]{1,0:T(8,128)S(1)} %convert_select_fusion), kind=kOutput, calls=%fused_computation.23 | convolution fusion | flops 537395200 | bytes 2627584 | tf_op jit(solution)/shard_map/dot_general | solution.py:112
  (5 shorter events, 0.1 us)
Async XLA Ops:
  0.0 3.8 %copy-start = (bf16[256,1024]{1,0:T(8,128)(2,1)S(1)}, bf16[256,1024]{1,0:T(8,128)(2,1)}, u32[]{:S(2)}) copy-start(bf16[256,1024]{1,0:T(8,128)(2,1)} %param.6) | copy-start | bytes 1572868
  7.0 41.1 %all-to-all-start = ((bf16[128,1,1,8,1024]{4,3,2,1,0:T(8,128)(2,1)}), bf16[128,1,1,8,1024]{4,3,2,1,0:T(8,128)(2,1)S(1)}, u32[]{:S(2)}, u32[]{:S(2)}) async-start(bf16[128,1,1,8,1024]{4,3,2,1,0:T(8,128)(2,1)} %copy.13), calls=%async_computation | async-start | bytes 4194304 | tf_op jit(solution)/shard_map/all_to_all | solution.py:26
  49.5 1.0 copy-start.1
where the time goes:
time: 110 us
  blocking collectives  34.1 us (31%)
  waiting for transfers between devices  28.5 us (26%)
  matrix products  28.1 us (26%)
  starting transfers between devices  11.5 us (10%)
  local copies, waits for them, and re-layouts  4.25 us (4%)
  other arithmetic  3.47 us (3%)
    all_to_all x1, blocking collectives, one_exchange(): lax.all_to_all(pieces, axis, split_axis=0, concat_axis=0, tiled=True)  34.1 us
    all_to_all x1, waiting for transfers between devices, one_exchange(): lax.all_to_all(pieces, axis, split_axis=0, concat_axis=0, tiled=True)  28.5 us
    dot_general x1, matrix products, expert_apply(): jnp.dot(hidden, w_down[0], preferred_element_type=jnp.float32)  13.4 us
    all_to_all x1, starting transfers between devices, one_exchange(): lax.all_to_all(pieces, axis, split_axis=0, concat_axis=0, tiled=True)  11.5 us
    dot_general x1, matrix products, expert_apply(): gate_pre = jnp.dot(row_block, w_gate[0], preferred_element_type=jnp.float32)  7.63 us
    dot_general x1, matrix products, compact_apply(): lax.dot_general(place_table, produced, (((0,), (0,)), ((), ())), preferre...  2.62 us
    another operation x1, local copies, waits for them, and re-layouts, one_exchange(): pieces = pieces.reshape(-1, *inside)  2.5 us
  transfers between devices with their start and end apart: 1, of which 1 were waited for; matrix products, arithmetic and copies ran while one was open for 1% of the time, Pallas kernels for 0%

commit v1 on v0

v1 whole, which is shorter than its diff:
```python
import jax
import jax.numpy as jnp
from jax import lax
from jax.experimental import pallas as pl
from jax.experimental.pallas import tpu as pltpu
from jax.sharding import PartitionSpec as P

PAIR = 8
SUB = 16
FF_TILES = ((0, 1024), (1024, 1024), (2048, 768))
MESH = pl.DeviceIdType.MESH
BF = jnp.bfloat16
F32 = jnp.float32


def partners(c, d, sign):
    g, l = lax.axis_index("grp"), lax.axis_index("loc")
    y, core = lax.div(g, 2), lax.rem(g, 2)
    x, z = lax.div(l, 4), lax.rem(l, 4)
    core2 = lax.rem(core + d, 2)
    if sign > 0:
        ys = [lax.rem(y + j, 4) * 2 + core2 for j in range(4)]
        xs = [lax.rem(x + j, 4) * 4 for j in range(4)]
        zs = [lax.rem(z + c + j, 4) for j in range(4)]
    else:
        ys = [lax.rem(y + 4 - j, 4) * 2 + core2 for j in range(4)]
        xs = [lax.rem(x + 4 - j, 4) * 4 for j in range(4)]
        zs = [lax.rem(z + 8 - c - j, 4) for j in range(4)]
    return [(ys[(a + b) % 4], xs[a] + zs[a]) for b in range(4) for a in range(4)]


def body(
    tokens_hbm, wg_hbm, wu_hbm, wd_hbm, chosen_hbm, weight_hbm, out_ref,
    tokens, wg, wu, wd, chosen, gates, upper, key, local, key2, select, spread, scale,
    send, recv, back, home, hidden, acc,
    in_sems, send_sem, recv_sems, back_sem, home_sems,
):
    n_dev, slots = chosen.shape
    n_tok, width = tokens.shape
    n_sub = n_dev // SUB
    rows = SUB * PAIR
    me = lax.axis_index("grp") * lax.axis_size("loc") + lax.axis_index("loc")

    def blocks(fn, sign):
        def step(s, _):
            d = lax.div(s, 4)
            fn(s, partners(s - 4 * d, d, sign))
            return 0

        lax.fori_loop(0, n_sub, step, 0)

    def skip_self(s, i, fn):
        if i == 0:
            pl.when(s > 0)(fn)
        else:
            fn()

    barrier = pltpu.get_barrier_semaphore()

    def greet(s, who):
        for i, w in enumerate(who):
            skip_self(s, i, lambda w=w: pl.semaphore_signal(barrier, inc=1, device_id=w, device_id_type=MESH))

    blocks(greet, 1)
    loads = [
        pltpu.make_async_copy(a, b, in_sems.at[i])
        for i, (a, b) in enumerate(
            ((chosen_hbm, chosen), (tokens_hbm, tokens), (weight_hbm, gates), (wg_hbm.at[0], wg), (wu_hbm.at[0], wu), (wd_hbm.at[0], wd))
        )
    ]
    for cp in loads:
        cp.start()

    row_i = lax.broadcasted_iota(jnp.int32, (slots, slots), 0)
    col_i = lax.broadcasted_iota(jnp.int32, (slots, slots), 1)
    upper[...] = jnp.where(row_i < col_i, 1.0, 0.0).astype(BF)
    pair_i = lax.broadcasted_iota(jnp.int32, (PAIR, slots), 0).astype(F32)
    token_i = (lax.broadcasted_iota(jnp.int32, (PAIR, n_tok), 1) + 1).astype(F32)

    def ranked(hit):
        ahead = jnp.dot(hit.astype(BF), upper[...], preferred_element_type=F32)
        return jnp.where(hit > 0.5, ahead, -1.0)

    loads[0].wait()
    picks = chosen[...]
    off = picks - me * n_tok
    mine = jnp.where((off >= 0) & (off < n_tok), 1.0, 0.0)
    key[...] = ranked(mine)
    local[...] = (off + 1).astype(F32)
    loads[1].wait()

    def build(s, who):
        for i, (g, l) in enumerate(who):
            e = g * lax.axis_size("loc") + l
            hit = key[pl.ds(e, 1), :] == pair_i
            where = jnp.sum(jnp.where(hit, local[pl.ds(e, 1), :], 0.0), axis=1, keepdims=True)
            select[pl.ds(pl.multiple_of(s * rows, rows) + i * PAIR, PAIR), :] = jnp.where(token_i == where, 1.0, 0.0)

    blocks(build, 1)

    def gather(s, _):
        block = select[pl.ds(pl.multiple_of(s * rows, rows), rows), :].astype(BF)
        picked = jnp.dot(block, tokens[...], preferred_element_type=F32)
        send[pl.ds(s * SUB, SUB)] = picked.reshape(SUB, PAIR, width).astype(BF)
        return 0

    lax.fori_loop(0, n_sub, gather, 0)
    recv[0] = send[0]
    pl.semaphore_wait(barrier, n_dev - 1)

    def dispatch(s, who):
        for i, w in enumerate(who):
            k = s * SUB + i
            skip_self(
                s, i,
                lambda k=k, w=w: pltpu.make_async_remote_copy(
                    send.at[k], recv.at[k], send_sem, recv_sems.at[s], device_id=w, device_id_type=MESH
                ).start(),
            )

    blocks(dispatch, 1)

    for s in range(n_sub):
        spread[:, s * rows : (s + 1) * rows] = select[s * rows : (s + 1) * rows, :].T.astype(BF)
    own = jnp.broadcast_to(chosen[pl.ds(me, 1), :], (n_dev, slots))
    low = lax.broadcasted_iota(jnp.int32, (n_dev, slots), 0) * n_tok
    key2[...] = ranked(jnp.where((own >= low) & (own < low + n_tok), 1.0, 0.0))
    loads[2].wait()
    own_gate = gates[pl.ds(me, 1), :]

    def weigh(s, who):
        for i, (g, l) in enumerate(who):
            e = g * lax.axis_size("loc") + l
            hit = key2[pl.ds(e, 1), :] == pair_i
            value = jnp.sum(jnp.where(hit, own_gate, 0.0), axis=1, keepdims=True)
            scale[pl.ds(pl.multiple_of(s * rows, rows) + i * PAIR, PAIR), :] = jnp.broadcast_to(value, (PAIR, scale.shape[1]))

    blocks(weigh, -1)
    for cp in loads[3:]:
        cp.wait()

    def got(sems, buf, s):
        @pl.when(s == 0)
        def _():
            ref = buf.at[pl.ds(1, SUB - 1)]
            pltpu.make_async_copy(ref, ref, sems.at[0]).wait()

        @pl.when(s > 0)
        def _():
            ref = buf.at[pl.ds(s * SUB, SUB)]
            pltpu.make_async_copy(ref, ref, sems.at[s]).wait()

    def expert(s, who):
        got(recv_sems, recv, s)
        x = recv[pl.ds(s * SUB, SUB)].astype(F32).reshape(rows, width).astype(BF)
        for start, size in FF_TILES:
            gate = jnp.dot(x, wg[:, start : start + size], preferred_element_type=F32)
            up = jnp.dot(x, wu[:, start : start + size], preferred_element_type=F32)
            hidden[:, start : start + size] = (gate / (1.0 + jnp.exp(-gate)) * up).astype(BF)
        made = jnp.dot(hidden[...], wd[...], preferred_element_type=F32)
        made = made * scale[pl.ds(pl.multiple_of(s * rows, rows), rows), :1]
        back[pl.ds(s * SUB, SUB)] = made.reshape(SUB, PAIR, width).astype(BF)
        for i, w in enumerate(who):
            k = s * SUB + i
            skip_self(
                s, i,
                lambda k=k, w=w: pltpu.make_async_remote_copy(
                    back.at[k], home.at[k], back_sem, home_sems.at[s], device_id=w, device_id_type=MESH
                ).start(),
            )

    blocks(expert, -1)
    home[0] = back[0]
    acc[...] = jnp.zeros_like(acc)

    def combine(s, _):
        got(home_sems, home, s)
        r = home[pl.ds(s * SUB, SUB)].astype(F32).reshape(rows, width).astype(BF)
        acc[...] += jnp.dot(spread[:, pl.ds(pl.multiple_of(s * rows, rows), rows)], r, preferred_element_type=F32)
        return 0

    lax.fori_loop(0, n_sub, combine, 0)
    out_ref[...] = acc[...].astype(out_ref.dtype)
    sent = send.at[pl.ds(1, n_dev - 1)]
    pltpu.make_async_copy(sent, sent, send_sem).wait()
    sent = back.at[pl.ds(1, n_dev - 1)]
    pltpu.make_async_copy(sent, sent, back_sem).wait()


def shards(tokens, w_gate, w_up, w_down, chosen, gate_weights):
    n_tok, width = tokens.shape
    n_dev, slots = chosen.shape
    ff = w_gate.shape[2]
    n_sub = n_dev // SUB
    any_space = pl.BlockSpec(memory_space=pl.ANY)
    total = n_dev * PAIR
    return pl.pallas_call(
        body,
        out_shape=jax.ShapeDtypeStruct((n_tok, width), BF),
        in_specs=[any_space] * 6,
        out_specs=pl.BlockSpec(memory_space=pltpu.VMEM),
        scratch_shapes=[
            pltpu.VMEM((n_tok, width), BF),
            pltpu.VMEM((width, ff), BF),
            pltpu.VMEM((width, ff), BF),
            pltpu.VMEM((ff, width), BF),
            pltpu.VMEM((n_dev, slots), jnp.int32),
            pltpu.VMEM((n_dev, slots), F32),
            pltpu.VMEM((slots, slots), BF),
            pltpu.VMEM((n_dev, slots), F32),
            pltpu.VMEM((n_dev, slots), F32),
            pltpu.VMEM((n_dev, slots), F32),
            pltpu.VMEM((total, n_tok), F32),
            pltpu.VMEM((n_tok, total), BF),
            pltpu.VMEM((total, 128), F32),
            pltpu.VMEM((n_dev, PAIR, width), BF),
            pltpu.VMEM((n_dev, PAIR, width), BF),
            pltpu.VMEM((n_dev, PAIR, width), BF),
            pltpu.VMEM((n_dev, PAIR, width), BF),
            pltpu.VMEM((SUB * PAIR, ff), BF),
            pltpu.VMEM((n_tok, width), F32),
            pltpu.SemaphoreType.DMA((6,)),
            pltpu.SemaphoreType.DMA,
            pltpu.SemaphoreType.DMA((n_sub,)),
            pltpu.SemaphoreType.DMA,
            pltpu.SemaphoreType.DMA((n_sub,)),
        ],
        compiler_params=pltpu.CompilerParams(
            collective_id=0, has_side_effects=True, vmem_limit_bytes=56 << 20
        ),
    )(tokens, w_gate, w_up, w_down, chosen, gate_weights)


def solution(mesh):
    return jax.shard_map(
        shards,
        mesh=mesh,
        in_specs=(
            P(("grp", "loc"), None),
            P(("grp", "loc"), None, None),
            P(("grp", "loc"), None, None),
            P(("grp", "loc"), None, None),
            P(),
            P(),
        ),
        out_specs=P(("grp", "loc"), None),
        check_vma=False,
    )
```

time: 110 us -> 63.7 us (0.58)
  Pallas kernels: 0 us -> 61.6 us
  blocking collectives: 34.1 us -> 0 us
  waiting for transfers between devices: 28.5 us -> 0 us
  matrix products: 28.1 us -> 0 us
  starting transfers between devices: 11.5 us -> 0 us
  other arithmetic: 3.47 us -> 0 us
  local copies, waits for them, and re-layouts: 4.25 us -> 1.87 us
    pallas_call x0 -> x1, Pallas kernels: none -> 61.6 us  [shards(): pl.pallas_call(body, out_shape=jax.ShapeDtypeStruct((n_tok, width), BF),...]
    all_to_all x1 -> x0, blocking collectives: 34.1 us -> none  [one_exchange(): lax.all_to_all(pieces, axis, split_axis=0, concat_axis=0, tiled=True)]
    all_to_all x1 -> x0, waiting for transfers between devices: 28.5 us -> none  [one_exchange(): lax.all_to_all(pieces, axis, split_axis=0, concat_axis=0, tiled=True)]
    dot_general x8 -> x0, matrix products: 28.1 us -> none  [the longest x1 13.4 us: expert_apply(): jnp.dot(hidden, w_down[0], preferred_element_type=jnp.float32)]
    all_to_all x1 -> x0, starting transfers between devices: 11.5 us -> none  [one_exchange(): lax.all_to_all(pieces, axis, split_axis=0, concat_axis=0, tiled=True)]
    another operation x1 -> x0, local copies, waits for them, and re-layouts: 2.5 us -> none  [one_exchange(): pieces = pieces.reshape(-1, *inside)]
    reduce_sum x1 -> x0, other arithmetic: 2 us -> none  [shards(): pick_weight = jnp.sum(rank_table * gate_weights[:, :, None], axis=1)]
    convert_element_type x1 -> x0, other arithmetic: 1.22 us -> none  [shards(): jnp.where(is_mine, chosen - device_id * token_count, 0).astype(jnp.float32)]
  transfers between devices with their start and end apart: 1 -> 0, of which waited for: 1 -> 0; matrix products, arithmetic and copies ran while one was open for 1% -> 0% of each run, Pallas kernels for 0% -> 0%
where the time goes in v1:
time: 63.7 us; the launch traced here: 63.5 us
  Pallas kernels  61.6 us (97%)
  local copies, waits for them, and re-layouts  1.87 us (3%)
    pallas_call x1, Pallas kernels, shards(): pl.pallas_call(body, out_shape=jax.ShapeDtypeStruct((n_tok, width), BF),...  61.6 us
    unnamed x1, local copies, waits for them, and re-layouts  1.87 us

profile of v1, /device:TPU:1, one launch (start us, length us, event | category | flops | bytes accessed | tf_op | source)
XLA Modules:
  0.0 63.5 jit_solution(14242411595601344197)
XLA Ops:
  0.0 61.6 %shard_map.64 = bf16[256,1024]{1,0:T(8,128)(2,1)} custom-call(bf16[256,1024]{1,0:T(8,128)(2,1)} %tokens_hbm.1, bf16[1,1024,2816]{2,1,0:T(8,128)(2,1)} %wg_hbm.1, bf16[1,1024,2816]{2,1,0:T(8,128)(2,1)} %wu_hbm.1, bf16[1,2816,1024]{2,1,0:T(8,128)(2,1)} %wd_hbm.1, s32[128,512]{1,0:T(8,128)} %chosen_hbm.1, f32[128,512]{1,0:T(8,128)} %weight_hbm.1), custom_call_target="tpu_custom_call" | custom-call | tf_op jit(solution)/shard_map/pallas_call | solution.py:197
  61.6 1.9 %copy.8 = bf16[256,1024]{1,0:T(8,128)(2,1)} copy(bf16[256,1024]{1,0:T(8,128)(2,1)} %shard_map.64) | data formatting | bytes 1048576

commit v2 on v1

--- a/solution.py
+++ b/solution.py
@@ -1,3 +1,5 @@
+import itertools
+
 import jax
 import jax.numpy as jnp
 from jax import lax
@@ -13,20 +15,30 @@
 F32 = jnp.float32
 
 
-def partners(c, d, sign):
-    g, l = lax.axis_index("grp"), lax.axis_index("loc")
-    y, core = lax.div(g, 2), lax.rem(g, 2)
-    x, z = lax.div(l, 4), lax.rem(l, 4)
-    core2 = lax.rem(core + d, 2)
-    if sign > 0:
-        ys = [lax.rem(y + j, 4) * 2 + core2 for j in range(4)]
-        xs = [lax.rem(x + j, 4) * 4 for j in range(4)]
-        zs = [lax.rem(z + c + j, 4) for j in range(4)]
-    else:
-        ys = [lax.rem(y + 4 - j, 4) * 2 + core2 for j in range(4)]
-        xs = [lax.rem(x + 4 - j, 4) * 4 for j in range(4)]
-        zs = [lax.rem(z + 8 - c - j, 4) for j in range(4)]
-    return [(ys[(a + b) % 4], xs[a] + zs[a]) for b in range(4) for a in range(4)]
+def by_link_load(offsets):
+    loads = {}
+    for o in offsets:
+        hops = []
+        for d in (o[0], o[2], o[3]):
+            hops += [1.0 if d in (1, 2) else 0.0, 1.0 if d in (2, 3) else 0.0]
+        loads[o] = hops
+    total = [sum(loads[o][i] for o in offsets) for i in range(6)]
+    left, done, out = list(offsets), [0.0] * 6, []
+    for n in range(len(offsets)):
+        goal = [(n + 1) * t / len(offsets) for t in total]
+        best = min(left, key=lambda o: sum((a + b - g) ** 2 for a, b, g in zip(done, loads[o], goal)))
+        done = [a + b for a, b in zip(done, loads[best])]
+        left.remove(best)
+        out.append(best)
+    return out
+
+
+OTHERS = [o for o in itertools.product(range(4), range(2), range(4), range(4)) if any(o)]
+ORDER = [(0, 0, 0, 0)] + by_link_load(OTHERS)
+
+
+def hops(o):
+    return sum(min(d, 4 - d) for d in (o[0], o[2], o[3]))
 
 
 def body(
@@ -40,28 +52,19 @@
     n_sub = n_dev // SUB
     rows = SUB * PAIR
     me = lax.axis_index("grp") * lax.axis_size("loc") + lax.axis_index("loc")
-
-    def blocks(fn, sign):
-        def step(s, _):
-            d = lax.div(s, 4)
-            fn(s, partners(s - 4 * d, d, sign))
-            return 0
-
-        lax.fori_loop(0, n_sub, step, 0)
-
-    def skip_self(s, i, fn):
-        if i == 0:
-            pl.when(s > 0)(fn)
-        else:
-            fn()
+    g, l = lax.axis_index("grp"), lax.axis_index("loc")
+    ys = [lax.rem(lax.div(g, 2) + j, 4) * 2 for j in range(4)]
+    cores = [lax.rem(g + j, 2) for j in range(2)]
+    xs = [lax.rem(lax.div(l, 4) + j, 4) * 4 for j in range(4)]
+    zs = [lax.rem(lax.rem(l, 4) + j, 4) for j in range(4)]
+
+    def partner(o, sign):
+        dy, dc, dx, dz = o
+        return ys[(sign * dy) % 4] + cores[dc], xs[(sign * dx) % 4] + zs[(sign * dz) % 4]
 
     barrier = pltpu.get_barrier_semaphore()
-
-    def greet(s, who):
-        for i, w in enumerate(who):
-            skip_self(s, i, lambda w=w: pl.semaphore_signal(barrier, inc=1, device_id=w, device_id_type=MESH))
-
-    blocks(greet, 1)
+    for o in sorted(OTHERS, key=hops, reverse=True):
+        pl.semaphore_signal(barrier, inc=1, device_id=partner(o, 1), device_id_type=MESH)
     loads = [
         pltpu.make_async_copy(a, b, in_sems.at[i])
         for i, (a, b) in enumerate(
@@ -89,36 +92,31 @@
     local[...] = (off + 1).astype(F32)
     loads[1].wait()
 
-    def build(s, who):
-        for i, (g, l) in enumerate(who):
-            e = g * lax.axis_size("loc") + l
+    def build(s):
+        for k in range(s * SUB, (s + 1) * SUB):
+            pg, pl_ = partner(ORDER[k], 1)
+            e = pg * lax.axis_size("loc") + pl_
             hit = key[pl.ds(e, 1), :] == pair_i
             where = jnp.sum(jnp.where(hit, local[pl.ds(e, 1), :], 0.0), axis=1, keepdims=True)
-            select[pl.ds(pl.multiple_of(s * rows, rows) + i * PAIR, PAIR), :] = jnp.where(token_i == where, 1.0, 0.0)
-
-    blocks(build, 1)
-
-    def gather(s, _):
-        block = select[pl.ds(pl.multiple_of(s * rows, rows), rows), :].astype(BF)
+            select[k * PAIR : (k + 1) * PAIR, :] = jnp.where(token_i == where, 1.0, 0.0)
+        block = select[s * rows : (s + 1) * rows, :].astype(BF)
         picked = jnp.dot(block, tokens[...], preferred_element_type=F32)
-        send[pl.ds(s * SUB, SUB)] = picked.reshape(SUB, PAIR, width).astype(BF)
-        return 0
-
-    lax.fori_loop(0, n_sub, gather, 0)
+        send[s * SUB : (s + 1) * SUB] = picked.reshape(SUB, PAIR, width).astype(BF)
+
+    def dispatch(first, last):
+        for k in range(first, last):
+            pltpu.make_async_remote_copy(
+                send.at[k], recv.at[k], send_sem, recv_sems.at[k // SUB],
+                device_id=partner(ORDER[k], 1), device_id_type=MESH,
+            ).start()
+
+    build(0)
     recv[0] = send[0]
     pl.semaphore_wait(barrier, n_dev - 1)
-
-    def dispatch(s, who):
-        for i, w in enumerate(who):
-            k = s * SUB + i
-            skip_self(
-                s, i,
-                lambda k=k, w=w: pltpu.make_async_remote_copy(
-                    send.at[k], recv.at[k], send_sem, recv_sems.at[s], device_id=w, device_id_type=MESH
-                ).start(),
-            )
-
-    blocks(dispatch, 1)
+    dispatch(1, SUB)
+    for s in range(1, n_sub):
+        build(s)
+        dispatch(s * SUB, (s + 1) * SUB)
 
     for s in range(n_sub):
         spread[:, s * rows : (s + 1) * rows] = select[s * rows : (s + 1) * rows, :].T.astype(BF)
@@ -128,14 +126,13 @@
     loads[2].wait()
     own_gate = gates[pl.ds(me, 1), :]
 
-    def weigh(s, who):
-        for i, (g, l) in enumerate(who):
-            e = g * lax.axis_size("loc") + l
-            hit = key2[pl.ds(e, 1), :] == pair_i
-            value = jnp.sum(jnp.where(hit, own_gate, 0.0), axis=1, keepdims=True)
-            scale[pl.ds(pl.multiple_of(s * rows, rows) + i * PAIR, PAIR), :] = jnp.broadcast_to(value, (PAIR, scale.shape[1]))
-
-    blocks(weigh, -1)
+    for k in range(n_dev):
+        pg, pl_ = partner(ORDER[k], -1)
+        e = pg * lax.axis_size("loc") + pl_
+        hit = key2[pl.ds(e, 1), :] == pair_i
+        value = jnp.sum(jnp.where(hit, own_gate, 0.0), axis=1, keepdims=True)
+        scale[k * PAIR : (k + 1) * PAIR, :] = jnp.broadcast_to(value, (PAIR, scale.shape[1]))
+
     for cp in loads[3:]:
         cp.wait()
 
@@ -150,7 +147,7 @@
             ref = buf.at[pl.ds(s * SUB, SUB)]
             pltpu.make_async_copy(ref, ref, sems.at[s]).wait()
 
-    def expert(s, who):
+    def expert(s, _):
         got(recv_sems, recv, s)
         x = recv[pl.ds(s * SUB, SUB)].astype(F32).reshape(rows, width).astype(BF)
         for start, size in FF_TILES:
@@ -160,27 +157,34 @@
         made = jnp.dot(hidden[...], wd[...], preferred_element_type=F32)
         made = made * scale[pl.ds(pl.multiple_of(s * rows, rows), rows), :1]
         back[pl.ds(s * SUB, SUB)] = made.reshape(SUB, PAIR, width).astype(BF)
-        for i, w in enumerate(who):
-            k = s * SUB + i
-            skip_self(
-                s, i,
-                lambda k=k, w=w: pltpu.make_async_remote_copy(
-                    back.at[k], home.at[k], back_sem, home_sems.at[s], device_id=w, device_id_type=MESH
-                ).start(),
-            )
-
-    blocks(expert, -1)
+        for j in range(n_sub):
+
+            @pl.when(s == j)
+            def _():
+                for k in range(max(j * SUB, 1), (j + 1) * SUB):
+                    pltpu.make_async_remote_copy(
+                        back.at[k], home.at[k], back_sem, home_sems.at[j],
+                        device_id=partner(ORDER[k], -1), device_id_type=MESH,
+                    ).start()
+
+        return 0
+
+    lax.fori_loop(0, n_sub, expert, 0)
     home[0] = back[0]
     acc[...] = jnp.zeros_like(acc)
 
-    def combine(s, _):
+    def part(s):
         got(home_sems, home, s)
         r = home[pl.ds(s * SUB, SUB)].astype(F32).reshape(rows, width).astype(BF)
-        acc[...] += jnp.dot(spread[:, pl.ds(pl.multiple_of(s * rows, rows), rows)], r, preferred_element_type=F32)
+        table = spread[:, pl.ds(pl.multiple_of(s * rows, rows), rows)]
+        return jnp.dot(table, r, preferred_element_type=F32)
+
+    def combine(s, _):
+        acc[...] += part(s)
         return 0
 
-    lax.fori_loop(0, n_sub, combine, 0)
-    out_ref[...] = acc[...].astype(out_ref.dtype)
+    lax.fori_loop(0, n_sub - 1, combine, 0)
+    out_ref[...] = (acc[...] + part(n_sub - 1)).astype(out_ref.dtype)
     sent = send.at[pl.ds(1, n_dev - 1)]
     pltpu.make_async_copy(sent, sent, send_sem).wait()
     sent = back.at[pl.ds(1, n_dev - 1)]
@@ -192,12 +196,11 @@
     n_dev, slots = chosen.shape
     ff = w_gate.shape[2]
     n_sub = n_dev // SUB
-    any_space = pl.BlockSpec(memory_space=pl.ANY)
     total = n_dev * PAIR
     return pl.pallas_call(
         body,
-        out_shape=jax.ShapeDtypeStruct((n_tok, width), BF),
-        in_specs=[any_space] * 6,
+        out_shape=pltpu.VMEM((n_tok, width), BF),
+        in_specs=[pl.BlockSpec(memory_space=pltpu.HBM)] * 6,
         out_specs=pl.BlockSpec(memory_space=pltpu.VMEM),
         scratch_shapes=[
             pltpu.VMEM((n_tok, width), BF),

time: 63.7 us -> 60.1 us (0.943)
  Pallas kernels: 61.6 us -> 59.2 us
  local copies, waits for them, and re-layouts: 1.87 us -> 0.8 us
    pallas_call x1, Pallas kernels: 61.6 us -> 59.2 us  [shards(): pl.pallas_call(body, out_shape=pltpu.VMEM((n_tok, width), BF), in_specs=[...]
    unnamed x1, local copies, waits for them, and re-layouts: 1.87 us -> 0.8 us
where the time goes in v2:
time: 60.1 us; the launch traced here: 60 us
  Pallas kernels  59.2 us (99%)
  local copies, waits for them, and re-layouts  0.8 us (1%)
    pallas_call x1, Pallas kernels, shards(): pl.pallas_call(body, out_shape=pltpu.VMEM((n_tok, width), BF), in_specs=[...  59.2 us

profile of v2, /device:TPU:1, one launch (start us, length us, event | category | flops | bytes accessed | tf_op | source)
XLA Modules:
  0.0 60.0 jit_solution(12127304669530171293)
XLA Ops:
  0.0 59.2 %shard_map.64 = bf16[256,1024]{1,0:T(8,128)(2,1)S(1)} custom-call(bf16[256,1024]{1,0:T(8,128)(2,1)} %tokens_hbm.1, bf16[1,1024,2816]{2,1,0:T(8,128)(2,1)} %wg_hbm.1, bf16[1,1024,2816]{2,1,0:T(8,128)(2,1)} %wu_hbm.1, bf16[1,2816,1024]{2,1,0:T(8,128)(2,1)} %wd_hbm.1, s32[128,512]{1,0:T(8,128)} %chosen_hbm.1, f32[128,512]{1,0:T(8,128)} %weight_hbm.1), custom_call_target="tpu_custom_call" | custom-call | tf_op jit(solution)/shard_map/pallas_call | solution.py:200
  59.2 0.8 %copy.8 = bf16[256,1024]{1,0:T(8,128)(2,1)} copy(bf16[256,1024]{1,0:T(8,128)(2,1)S(1)} %shard_map.64) | data formatting | bytes 1048576

commit v3 on v2

--- a/solution.py
+++ b/solution.py
@@ -7,6 +7,7 @@
 from jax.experimental.pallas import tpu as pltpu
 from jax.sharding import PartitionSpec as P
 
+N_FIRST = 19
 PAIR = 8
 SUB = 16
 FF_TILES = ((0, 1024), (1024, 1024), (2048, 768))
@@ -34,7 +35,16 @@
 
 
 OTHERS = [o for o in itertools.product(range(4), range(2), range(4), range(4)) if any(o)]
-ORDER = [(0, 0, 0, 0)] + by_link_load(OTHERS)
+
+
+def lines_left(o):
+    return (o[:2] != (0, 0)) + (o[2] > 0) + (o[3] > 0)
+
+
+NEAR = [o for o in OTHERS if lines_left(o) < 3]
+X_LINE = [o for o in OTHERS if o[2] > 0 and lines_left(o) == 1]
+FIRST = by_link_load(sorted(NEAR, key=lines_left)[:N_FIRST])
+ORDER = [(0, 0, 0, 0)] + FIRST + by_link_load([o for o in OTHERS if o not in FIRST])
 
 
 def hops(o):
@@ -45,7 +55,7 @@
     tokens_hbm, wg_hbm, wu_hbm, wd_hbm, chosen_hbm, weight_hbm, out_ref,
     tokens, wg, wu, wd, chosen, gates, upper, key, local, key2, select, spread, scale,
     send, recv, back, home, hidden, acc,
-    in_sems, send_sem, recv_sems, back_sem, home_sems,
+    in_sems, send_sem, recv_sems, back_sem, home_sems, far_sem,
 ):
     n_dev, slots = chosen.shape
     n_tok, width = tokens.shape
@@ -63,7 +73,7 @@
         return ys[(sign * dy) % 4] + cores[dc], xs[(sign * dx) % 4] + zs[(sign * dz) % 4]
 
     barrier = pltpu.get_barrier_semaphore()
-    for o in sorted(OTHERS, key=hops, reverse=True):
+    for o in sorted(NEAR, key=hops, reverse=True):
         pl.semaphore_signal(barrier, inc=1, device_id=partner(o, 1), device_id_type=MESH)
     loads = [
         pltpu.make_async_copy(a, b, in_sems.at[i])
@@ -112,11 +122,18 @@
 
     build(0)
     recv[0] = send[0]
-    pl.semaphore_wait(barrier, n_dev - 1)
+    pl.semaphore_wait(barrier, len(NEAR))
+    for o in X_LINE:
+        pl.semaphore_signal(far_sem, inc=1, device_id=partner(o, 1), device_id_type=MESH)
     dispatch(1, SUB)
     for s in range(1, n_sub):
         build(s)
-        dispatch(s * SUB, (s + 1) * SUB)
+        first, last, known = s * SUB, (s + 1) * SUB, len(FIRST) + 1
+        if first <= known < last:
+            dispatch(first, known)
+            pl.semaphore_wait(far_sem, len(X_LINE))
+            first = known
+        dispatch(first, last)
 
     for s in range(n_sub):
         spread[:, s * rows : (s + 1) * rows] = select[s * rows : (s + 1) * rows, :].T.astype(BF)
@@ -227,6 +244,7 @@
             pltpu.SemaphoreType.DMA((n_sub,)),
             pltpu.SemaphoreType.DMA,
             pltpu.SemaphoreType.DMA((n_sub,)),
+            pltpu.SemaphoreType.REGULAR,
         ],
         compiler_params=pltpu.CompilerParams(
             collective_id=0, has_side_effects=True, vmem_limit_bytes=56 << 20

time: 60.1 us -> 58.8 us (0.978)
  Pallas kernels: 59.2 us -> 57.9 us
    pallas_call x1, Pallas kernels: 59.2 us -> 57.9 us  [shards(): pl.pallas_call(body, out_shape=pltpu.VMEM((n_tok, width), BF), in_specs=[...]
where the time goes in v3:
time: 58.8 us; the launch traced here: 58.7 us
  Pallas kernels  57.9 us (98%)
  local copies, waits for them, and re-layouts  0.8 us (1%)
    pallas_call x1, Pallas kernels, shards(): pl.pallas_call(body, out_shape=pltpu.VMEM((n_tok, width), BF), in_specs=[...  57.9 us

profile of v3, /device:TPU:1, one launch (start us, length us, event | category | flops | bytes accessed | tf_op | source)
XLA Modules:
  0.0 58.7 jit_solution(3372224834023861202)
XLA Ops:
  0.0 57.9 %shard_map.64 = bf16[256,1024]{1,0:T(8,128)(2,1)S(1)} custom-call(bf16[256,1024]{1,0:T(8,128)(2,1)} %tokens_hbm.1, bf16[1,1024,2816]{2,1,0:T(8,128)(2,1)} %wg_hbm.1, bf16[1,1024,2816]{2,1,0:T(8,128)(2,1)} %wu_hbm.1, bf16[1,2816,1024]{2,1,0:T(8,128)(2,1)} %wd_hbm.1, s32[128,512]{1,0:T(8,128)} %chosen_hbm.1, f32[128,512]{1,0:T(8,128)} %weight_hbm.1), custom_call_target="tpu_custom_call" | custom-call | tf_op jit(solution)/shard_map/pallas_call | solution.py:217
  57.9 0.8 %copy.8 = bf16[256,1024]{1,0:T(8,128)(2,1)} copy(bf16[256,1024]{1,0:T(8,128)(2,1)S(1)} %shard_map.64) | data formatting | bytes 1048576

commit v4 on v3

--- a/solution.py
+++ b/solution.py
@@ -72,16 +72,18 @@
         dy, dc, dx, dz = o
         return ys[(sign * dy) % 4] + cores[dc], xs[(sign * dx) % 4] + zs[(sign * dz) % 4]
 
-    barrier = pltpu.get_barrier_semaphore()
-    for o in sorted(NEAR, key=hops, reverse=True):
-        pl.semaphore_signal(barrier, inc=1, device_id=partner(o, 1), device_id_type=MESH)
     loads = [
         pltpu.make_async_copy(a, b, in_sems.at[i])
         for i, (a, b) in enumerate(
             ((chosen_hbm, chosen), (tokens_hbm, tokens), (weight_hbm, gates), (wg_hbm.at[0], wg), (wu_hbm.at[0], wu), (wd_hbm.at[0], wd))
         )
     ]
-    for cp in loads:
+    for cp in loads[:2]:
+        cp.start()
+    barrier = pltpu.get_barrier_semaphore()
+    for o in sorted(NEAR, key=hops, reverse=True):
+        pl.semaphore_signal(barrier, inc=1, device_id=partner(o, 1), device_id_type=MESH)
+    for cp in loads[2:]:
         cp.start()
 
     row_i = lax.broadcasted_iota(jnp.int32, (slots, slots), 0)
@@ -188,7 +190,6 @@
 
     lax.fori_loop(0, n_sub, expert, 0)
     home[0] = back[0]
-    acc[...] = jnp.zeros_like(acc)
 
     def part(s):
         got(home_sems, home, s)
@@ -200,7 +201,8 @@
         acc[...] += part(s)
         return 0
 
-    lax.fori_loop(0, n_sub - 1, combine, 0)
+    acc[...] = part(0)
+    lax.fori_loop(1, n_sub - 1, combine, 0)
     out_ref[...] = (acc[...] + part(n_sub - 1)).astype(out_ref.dtype)
     sent = send.at[pl.ds(1, n_dev - 1)]
     pltpu.make_async_copy(sent, sent, send_sem).wait()

time: 58.8 us -> 58.8 us (level)
  no operation moved by 1% of the time
where the time goes in v4:
time: 58.8 us; the launch traced here: 58.7 us
  Pallas kernels  57.9 us (98%)
  local copies, waits for them, and re-layouts  0.8 us (1%)
    pallas_call x1, Pallas kernels, shards(): pl.pallas_call(body, out_shape=pltpu.VMEM((n_tok, width), BF), in_specs=[...  57.9 us

profile of v4, /device:TPU:1, one launch (start us, length us, event | category | flops | bytes accessed | tf_op | source)
XLA Modules:
  0.0 58.7 jit_solution(15626847262216818629)
XLA Ops:
  0.0 57.9 %shard_map.64 = bf16[256,1024]{1,0:T(8,128)(2,1)S(1)} custom-call(bf16[256,1024]{1,0:T(8,128)(2,1)} %tokens_hbm.1, bf16[1,1024,2816]{2,1,0:T(8,128)(2,1)} %wg_hbm.1, bf16[1,1024,2816]{2,1,0:T(8,128)(2,1)} %wu_hbm.1, bf16[1,2816,1024]{2,1,0:T(8,128)(2,1)} %wd_hbm.1, s32[128,512]{1,0:T(8,128)} %chosen_hbm.1, f32[128,512]{1,0:T(8,128)} %weight_hbm.1), custom_call_target="tpu_custom_call" | custom-call | tf_op jit(solution)/shard_map/pallas_call | solution.py:219
  57.9 0.8 %copy.8 = bf16[256,1024]{1,0:T(8,128)(2,1)} copy(bf16[256,1024]{1,0:T(8,128)(2,1)S(1)} %shard_map.64) | data formatting | bytes 1048576

commit v5 on v3

--- a/solution.py
+++ b/solution.py
@@ -81,7 +81,7 @@
             ((chosen_hbm, chosen), (tokens_hbm, tokens), (weight_hbm, gates), (wg_hbm.at[0], wg), (wu_hbm.at[0], wu), (wd_hbm.at[0], wd))
         )
     ]
-    for cp in loads:
+    for cp in loads[:3]:
         cp.start()
 
     row_i = lax.broadcasted_iota(jnp.int32, (slots, slots), 0)
@@ -122,6 +122,8 @@
 
     build(0)
     recv[0] = send[0]
+    for cp in loads[3:]:
+        cp.start()
     pl.semaphore_wait(barrier, len(NEAR))
     for o in X_LINE:
         pl.semaphore_signal(far_sem, inc=1, device_id=partner(o, 1), device_id_type=MESH)

time: 58.8 us -> 58.8 us (level)
  no operation moved by 1% of the time
where the time goes in v5:
time: 58.8 us; the launch traced here: 58.7 us
  Pallas kernels  57.9 us (98%)
  local copies, waits for them, and re-layouts  0.8 us (1%)
    pallas_call x1, Pallas kernels, shards(): pl.pallas_call(body, out_shape=pltpu.VMEM((n_tok, width), BF), in_specs=[...  57.9 us

profile of v5, /device:TPU:1, one launch (start us, length us, event | category | flops | bytes accessed | tf_op | source)
XLA Modules:
  0.0 58.7 jit_solution(4066363649851809874)
XLA Ops:
  0.0 57.9 %shard_map.64 = bf16[256,1024]{1,0:T(8,128)(2,1)S(1)} custom-call(bf16[256,1024]{1,0:T(8,128)(2,1)} %tokens_hbm.1, bf16[1,1024,2816]{2,1,0:T(8,128)(2,1)} %wg_hbm.1, bf16[1,1024,2816]{2,1,0:T(8,128)(2,1)} %wu_hbm.1, bf16[1,2816,1024]{2,1,0:T(8,128)(2,1)} %wd_hbm.1, s32[128,512]{1,0:T(8,128)} %chosen_hbm.1, f32[128,512]{1,0:T(8,128)} %weight_hbm.1), custom_call_target="tpu_custom_call" | custom-call | tf_op jit(solution)/shard_map/pallas_call | solution.py:219
  57.9 0.8 %copy.8 = bf16[256,1024]{1,0:T(8,128)(2,1)} copy(bf16[256,1024]{1,0:T(8,128)(2,1)S(1)} %shard_map.64) | data formatting | bytes 1048576
